TPU v7x, 32 devices: a whole 2x2x4 slice. The times are simulated.
32 devices in a mesh: fsdp: 2 (over y), tensor: 16 (over z, x, core).
Axes of the slice: x: 2, y: 2, z: 4, core: 2. Of those that a mesh axis runs over, the one named last changes fastest.
Arguments:
- momentum: bfloat16 [8192, 28672], P('fsdp', 'tensor'), may hold values from -6 to 6
- gradient: bfloat16 [8192, 28672], P('fsdp', 'tensor'), may hold values from -4 to 4
- factor: float32 [28672, 512], P('tensor', 'fsdp'), may hold values from -0.03125 to 0.03125
Outputs:
- new_momentum: bfloat16 [8192, 28672], P('fsdp', 'tensor')
- new_factor: float32 [28672, 512], P('tensor', 'fsdp')
- update: bfloat16 [8192, 28672], P('fsdp', 'tensor')
All inputs are finite; a program needn't handle non-finite values.
Results may differ from a plain program's by a relative error of at most 0.017.
Values may be sent and summed in bfloat16 or wider, within the bound.
A program may use at most 128 MiB of HBM per device.

v0:
```python
import jax
import jax.numpy as jnp
from jax import lax
from jax.experimental import pallas as pl
from jax.experimental.pallas import tpu as pltpu
from jax.sharding import PartitionSpec as P

decay_rate = 0.95
epsilon = 1e-06
BLOCK = 128


def inverse_kernel(gram_ref, out_ref, state):
    rank = gram_ref.shape[0]
    rows = lax.broadcasted_iota(jnp.int32, (rank, rank), 0)
    columns = lax.broadcasted_iota(jnp.int32, (rank, rank), 1)
    state[:, :rank] = gram_ref[...]
    state[:, rank:] = (rows == columns).astype(jnp.float32)
    r_in = lax.broadcasted_iota(jnp.int32, (BLOCK, BLOCK), 0)
    c_in = lax.broadcasted_iota(jnp.int32, (BLOCK, BLOCK), 1)
    wide = lax.broadcasted_iota(jnp.int32, (BLOCK, rank), 1)

    @pl.loop(0, rank // BLOCK)
    def _(b):
        at = pl.multiple_of(b * BLOCK, BLOCK)
        a = state[pl.ds(at, BLOCK), pl.ds(at, BLOCK)]
        v = (r_in == c_in).astype(jnp.float32)
        for j in range(BLOCK - 1):
            lo = (j + 1) // 8 * 8
            top = a[lo:, :]
            scale = 1.0 / a[j : j + 1, j : j + 1]
            factor = jnp.where(r_in[lo:, :1] > j, top[:, j : j + 1] * scale, 0.0)
            new_a = top - factor * a[j : j + 1, :]
            new_v = v[lo:, :] - factor * v[j : j + 1, :]
            a = new_a if lo == 0 else jnp.concatenate([a[:lo], new_a], axis=0)
            v = new_v if lo == 0 else jnp.concatenate([v[:lo], new_v], axis=0)
        diagonal = jnp.sum(jnp.where(r_in == c_in, a, 0.0), axis=1, keepdims=True)
        block_inverse = v * (1.0 / jnp.sqrt(diagonal))
        solved = jnp.dot(
            block_inverse,
            state[pl.ds(at, BLOCK), :],
            precision=lax.Precision.HIGHEST,
            preferred_element_type=jnp.float32,
        )
        out_ref[pl.ds(at, BLOCK), :] = solved[:, rank:]
        lower = jnp.where(wide >= at + BLOCK, solved[:, :rank], 0.0)
        state[...] = state[...] - lax.dot_general(
            lower,
            solved,
            (((0,), (0,)), ((), ())),
            precision=lax.Precision.HIGHEST,
            preferred_element_type=jnp.float32,
        )


def inverse_of_lower(gram):
    rank = gram.shape[0]
    return pl.pallas_call(
        inverse_kernel,
        out_shape=jax.ShapeDtypeStruct((rank, rank), jnp.float32),
        in_specs=[pl.BlockSpec(memory_space=pltpu.VMEM)],
        out_specs=pl.BlockSpec(memory_space=pltpu.VMEM),
        scratch_shapes=[pltpu.VMEM((rank, 2 * rank), jnp.float32)],
        compiler_params=pltpu.CompilerParams(vmem_limit_bytes=32 << 20),
        cost_estimate=pl.CostEstimate(flops=40_000_000_000, bytes_accessed=2 << 20, transcendentals=0),
    )(gram)


def butterfly(value, axis, size):
    if size & (size - 1):
        return lax.psum(value, axis)
    step = 1
    while step < size:
        value = value + lax.ppermute(value, axis, [(i, i ^ step) for i in range(size)])
        step *= 2
    return value


def on_device(halves, spread, momentum, gradient, factor):
    whole_rows = momentum.shape[0] * halves
    whole_columns = momentum.shape[1] * spread
    own_rank = factor.shape[1]
    rank = own_rank * halves
    place = lax.axis_index("fsdp")
    swap = [(0, 1), (1, 0)]

    blended = (momentum.astype(jnp.float32) + gradient.astype(jnp.float32)).astype(jnp.bfloat16)
    lowered = factor.astype(jnp.bfloat16)

    def summed_rows(columns):
        part = jnp.dot(blended, columns, preferred_element_type=jnp.float32).astype(jnp.bfloat16)
        return lax.psum_scatter(part, "tensor", scatter_dimension=0, tiled=True)

    if halves == 2:
        other = lax.ppermute(lowered, "fsdp", swap)
        mine = summed_rows(lowered)
        theirs = summed_rows(other)
        rows = jnp.where(
            place == 0,
            jnp.concatenate([mine, theirs], axis=1),
            jnp.concatenate([theirs, mine], axis=1),
        )
    else:
        rows = summed_rows(lax.all_gather(lowered, "fsdp", axis=1, tiled=True))

    gram = lax.psum(
        lax.dot_general(rows, rows, (((0,), (0,)), ((), ())), preferred_element_type=jnp.float32),
        ("fsdp", "tensor"),
    )
    left = lax.all_gather(rows, "tensor", axis=0, tiled=True)
    lower_inverse = inverse_of_lower(gram)
    high = lower_inverse.astype(jnp.bfloat16)
    low = (lower_inverse - high.astype(jnp.float32)).astype(jnp.bfloat16)
    across = (((1,), (1,)), ((), ()))
    orthonormal = (
        lax.dot_general(left, high, across, preferred_element_type=jnp.float32)
        + lax.dot_general(left, low, across, preferred_element_type=jnp.float32)
    ).astype(jnp.bfloat16)

    share = lax.dot_general(
        orthonormal, blended, (((0,), (0,)), ((), ())), preferred_element_type=jnp.float32
    ).astype(jnp.bfloat16)
    if halves == 2:
        right = share.astype(jnp.float32) + lax.ppermute(share, "fsdp", swap).astype(jnp.float32)
    else:
        right = lax.psum(share, "fsdp").astype(jnp.float32)
    square_sums = butterfly(jnp.sum(right * right, axis=1), "tensor", spread)
    inverse = lax.rsqrt(square_sums + epsilon)
    normal = right * inverse[:, None]
    own_factor = lax.dynamic_slice_in_dim(normal, place * own_rank, own_rank, axis=0).T
    product = jnp.dot(orthonormal, right.astype(jnp.bfloat16), preferred_element_type=jnp.float32)
    new_momentum = (blended.astype(jnp.float32) - (1.0 - decay_rate) * product).astype(jnp.bfloat16)
    stepped = jnp.dot(orthonormal, normal.astype(jnp.bfloat16), preferred_element_type=jnp.float32)
    scale = jnp.sqrt(jnp.float32(whole_rows * whole_columns / rank))
    update = (stepped * scale).astype(jnp.bfloat16)
    return (new_momentum, own_factor, update)


def solution(mesh):
    halves, spread = mesh.shape["fsdp"], mesh.shape["tensor"]

    def body(momentum, gradient, factor):
        return on_device(halves, spread, momentum, gradient, factor)

    return jax.shard_map(
        body,
        mesh=mesh,
        in_specs=(P("fsdp", "tensor"), P("fsdp", "tensor"), P("tensor", "fsdp")),
        out_specs=(P("fsdp", "tensor"), P("tensor", "fsdp"), P("fsdp", "tensor")),
        check_vma=False,
    )
```

profile of v0, /device:TPU:0, one launch (start us, length us, event | category | flops | bytes accessed | tf_op | source)
XLA Modules:
  0.0 461.5 jit_solution(949954754372182483)
XLA Ops:
  7.2 1.6 convert_element_type.58
  8.8 11.6 %add_convert_fusion = bf16[4096,1792]{1,0:T(8,128)(2,1)S(1)} fusion(bf16[4096,1792]{1,0:T(8,128)(2,1)} %param.4, bf16[4096,1792]{1,0:T(8,128)(2,1)} %param.3), kind=kLoop, calls=%fused_computation.2 | loop fusion | flops 29360128 | bytes 44040192 | tf_op jit(solution)/shard_map/convert_element_type | solution.py:87
  20.4 5.5 %copy-done.2 = bf16[4096,1792]{1,0:T(8,128)(2,1)} copy-done((bf16[4096,1792]{1,0:T(8,128)(2,1)}, bf16[4096,1792]{1,0:T(8,128)(2,1)S(1)}, u32[]{:S(2)}) %copy-start.2) | copy-done | bytes 14680088
  25.9 5.3 %convolution_convert_fusion.1 = bf16[4096,256]{1,0:T(8,128)(2,1)} fusion(bf16[4096,1792]{1,0:T(8,128)(2,1)S(1)} %add_convert_fusion, bf16[1792,256]{1,0:T(8,128)(2,1)S(1)} %convert_element_type.58), kind=kOutput, calls=%fused_computation.5 | convolution fusion | flops 3759144960 | bytes 17694720 | tf_op jit(solution)/shard_map/dot_general | solution.py:91
  31.3 3.1 collective-permute-start
  34.3 20.4 %collective-permute-done = bf16[1792,256]{1,0:T(8,128)(2,1)S(1)} collective-permute-done((bf16[1792,256]{1,0:T(8,128)(2,1)S(1)}, bf16[1792,256]{1,0:T(8,128)(2,1)S(1)}, u32[]{:S(2)}, u32[]{:S(2)}) %collective-permute-start) | collective-permute-done | bytes 917536 | tf_op jit(solution)/shard_map/ppermute | solution.py:95
  54.7 10.5 %convolution_convert_fusion = bf16[4096,256]{1,0:T(8,128)(2,1)} fusion(bf16[4096,1792]{1,0:T(8,128)(2,1)} %copy-done.2, bf16[1792,256]{1,0:T(8,128)(2,1)S(1)} %collective-permute-done), kind=kOutput, calls=%fused_computation.4 | convolution fusion | flops 3759144960 | bytes 17694720 | tf_op jit(solution)/shard_map/dot_general | solution.py:91
  65.3 30.7 %reduce-scatter.3.cloned.1.call-done = bf16[256,256]{1,0:T(8,128)(2,1)} async-done(((bf16[4096,256]{1,0:T(8,128)(2,1)}), bf16[256,256]{1,0:T(8,128)(2,1)}) %reduce-scatter.3.cloned.1.call-update) | async-done | bytes 131088 | tf_op jit(solution)/shard_map/reduce_scatter | solution.py:92
  95.9 65.1 %reduce-scatter.5.cloned.1.call-done = bf16[256,256]{1,0:T(8,128)(2,1)} async-done(((bf16[4096,256]{1,0:T(8,128)(2,1)}), bf16[256,256]{1,0:T(8,128)(2,1)}) %reduce-scatter.5.cloned.1.call-update) | async-done | bytes 131088 | tf_op jit(solution)/shard_map/reduce_scatter | solution.py:92
  161.0 1.2 maximum_select_fusion
  162.2 1.3 fusion.7
  164.1 132.3 %all-reduce.2.cloned.1.call-done.gram_ref = f32[512,512]{1,0:T(8,128)} async-done(((f32[512,512]{1,0:T(8,128)}), f32[512,512]{1,0:T(8,128)}) %all-reduce.2.cloned.1.call-update) | async-done | bytes 1048592 | tf_op jit(solution)/shard_map/psum | solution.py:106
  296.4 1.2 copy-done
  297.6 51.8 %shard_map.58 = f32[512,512]{1,0:T(8,128)S(1)} custom-call(f32[512,512]{1,0:T(8,128)S(1)} %copy-done), custom_call_target="tpu_custom_call" | custom-call | flops 40000000000 | bytes 2097152 | tf_op jit(solution)/shard_map/pallas_call | solution.py:58
  349.4 4.9 %fusion.5 = f32[4096,512]{1,0:T(8,128)S(1)} fusion(bf16[4096,512]{1,0:T(8,128)(2,1)} %all-gather.2.cloned.1.call-done, f32[512,512]{1,0:T(8,128)S(1)} %shard_map.58), kind=kOutput, calls=%fused_computation.16 | convolution fusion | flops 2147745792 | bytes 13631488 | tf_op jit(solution)/shard_map/dot_general | solution.py:116
  354.4 2.5 add_convert_fusion.1
  356.9 13.8 %convolution_convert_fusion.2 = bf16[512,1792]{1,0:T(8,128)(2,1)S(1)} fusion(bf16[4096,512]{1,0:T(8,128)(2,1)S(1)} %add_convert_fusion.1, bf16[4096,1792]{1,0:T(8,128)(2,1)} %copy-done.2), kind=kOutput, calls=%fused_computation.10 | convolution fusion | flops 7517110272 | bytes 20709376 | tf_op jit(solution)/shard_map/dot_general | solution.py:120
  370.6 1.5 collective-permute-start.1
  372.2 40.0 %collective-permute-done.1 = bf16[512,1792]{1,0:T(8,128)(2,1)S(1)} collective-permute-done((bf16[512,1792]{1,0:T(8,128)(2,1)S(1)}, bf16[512,1792]{1,0:T(8,128)(2,1)S(1)}, u32[]{:S(2)}, u32[]{:S(2)}) %collective-permute-start.1) | collective-permute-done | bytes 1835040 | tf_op jit(solution)/shard_map/ppermute | solution.py:124
  412.1 1.2 copy-done.5
  413.3 0.7 multiply_reduce_fusion
  414.1 1.1 collective-permute-done.2
  415.2 1.0 collective-permute-start.3
  416.2 2.6 collective-permute-done.3
  418.8 1.5 collective-permute-start.4
  420.3 2.1 collective-permute-done.4
  422.4 1.8 collective-permute-start.5
  424.2 15.7 %subtract_convert_fusion = bf16[4096,1792]{1,0:T(8,128)(2,1)} fusion(bf16[4096,1792]{1,0:T(8,128)(2,1)} %copy-done.2, bf16[4096,512]{1,0:T(8,128)(2,1)} %copy-done.3, bf16[512,1792]{1,0:T(8,128)(2,1)} %copy-done.5, bf16[512,1792]{1,0:T(8,128)(2,1)S(1)} %convolution_convert_fusion.2), kind=kOutput, calls=%fused_computation.1 | convolution fusion | flops 7549222912 | bytes 37224448 | tf_op jit(solution)/shard_map/dot_general | solution.py:131
  439.9 2.2 fusion
  442.1 0.6 copy-done.4
  442.6 10.5 %multiply_convert_fusion = bf16[4096,1792]{1,0:T(8,128)(2,1)} fusion(bf16[4096,512]{1,0:T(8,128)(2,1)S(1)} %copy-done.4, f32[512,1792]{1,0:T(8,128)S(1)} %fusion), kind=kOutput, calls=%fused_computation | convolution fusion | flops 7531790336 | bytes 22544384 | tf_op jit(solution)/shard_map/dot_general | solution.py:133
  453.3 1.7 copy.6
  (26 shorter events, 1.0 us)
Async XLA Ops:
  7.2 88.7 %reduce-scatter.3.cloned.1.call-start = ((), (), s32[]{:S(2)}) async-start(), calls=%async_computation.2 | async-start | bytes 2228224 | tf_op jit(solution)/shard_map/reduce_scatter | solution.py:92
  20.4 5.5 %copy-start.2 = (bf16[4096,1792]{1,0:T(8,128)(2,1)}, bf16[4096,1792]{1,0:T(8,128)(2,1)S(1)}, u32[]{:S(2)}) copy-start(bf16[4096,1792]{1,0:T(8,128)(2,1)S(1)} %add_convert_fusion) | copy-start | bytes 44040196
  31.2 129.8 %reduce-scatter.5.cloned.1.call-start = ((), (), s32[]{:S(2)}) async-start(), calls=%async_computation.3 | async-start | bytes 2228224 | tf_op jit(solution)/shard_map/reduce_scatter | solution.py:92
  31.3 23.4 %collective-permute-start = (bf16[1792,256]{1,0:T(8,128)(2,1)S(1)}, bf16[1792,256]{1,0:T(8,128)(2,1)S(1)}, u32[]{:S(2)}, u32[]{:S(2)}) collective-permute-start(bf16[1792,256]{1,0:T(8,128)(2,1)S(1)} %convert_element_type.58), channel_id=1, source_target_pairs={{0,16},{16,0},{1,17},{17,1},{2,18},{18,2},{3,19},{19,3},{4,20},{20... | collective-permute-start | bytes 2752520 | tf_op jit(solution)/shard_map/ppermute | solution.py:95
  65.2 231.2 %all-reduce.2.cloned.1.call-start = ((), (), s32[]{:S(2)}) async-start(), calls=%async_computation.5 | async-start | bytes 2097152 | tf_op jit(solution)/shard_map/psum | solution.py:106
  162.2 1.6 copy-start.6
  163.5 185.9 %all-gather.2.cloned.1.call-start = ((), (), s32[]{:S(2)}) async-start(), calls=%async_computation.4 | async-start | bytes 4456448 | tf_op jit(solution)/shard_map/all_gather | solution.py:110
  296.4 1.2 copy-start
  349.4 4.9 %copy-start.1 = (bf16[4096,512]{1,0:T(8,128)(2,1)S(1)}, bf16[4096,512]{1,0:T(8,128)(2,1)}, u32[]{:S(2)}) copy-start(bf16[4096,512]{1,0:T(8,128)(2,1)} %all-gather.2.cloned.1.call-done) | copy-start | bytes 12582916
  356.8 13.8 %copy-start.3 = (bf16[4096,512]{1,0:T(8,128)(2,1)}, bf16[4096,512]{1,0:T(8,128)(2,1)S(1)}, u32[]{:S(2)}) copy-start(bf16[4096,512]{1,0:T(8,128)(2,1)S(1)} %add_convert_fusion.1) | copy-start | bytes 12582916
  370.6 41.5 %collective-permute-start.1 = (bf16[512,1792]{1,0:T(8,128)(2,1)S(1)}, bf16[512,1792]{1,0:T(8,128)(2,1)S(1)}, u32[]{:S(2)}, u32[]{:S(2)}) collective-permute-start(bf16[512,1792]{1,0:T(8,128)(2,1)S(1)} %convolution_convert_fusion.2), channel_id=1, source_target_pairs={{0,16},{16,0},{1,17},{17,1},{2,18},{18,2},{3,19},{19,3},{4,20},{20... | collective-permute-start | bytes 5505032 | tf_op jit(solution)/shard_map/ppermute | solution.py:124
  412.1 1.2 copy-start.5
  414.0 1.2 collective-permute-start.2
  415.2 3.6 collective-permute-start.3
  418.8 3.6 collective-permute-start.4
  422.4 17.4 %collective-permute-start.5 = (f32[512]{0:T(512)S(1)}, f32[512]{0:T(512)S(1)}, u32[]{:S(2)}, u32[]{:S(2)}) collective-permute-start(f32[512]{0:T(512)S(1)} %add.41), channel_id=1, source_target_pairs={{0,8},{1,9},{2,10},{3,11},{4,12},{5,13},{6,14},{7,15},{8,0},{9,1},... | collective-permute-start | bytes 6152 | tf_op jit(solution)/shard_map/ppermute | solution.py:74
  439.9 2.7 copy-start.4
Sparse Core Ops, SparseCore 0:
  31.3 64.5 reduce-scatter.2
  100.2 60.7 reduce-scatter.4
  166.8 129.5 all-reduce.1
  299.0 49.6 all-gather.1
where the time goes:
time: 462 us; the launch traced here: 461 us
  waiting for transfers between devices  295 us (64%)
  matrix products  64.4 us (14%)
  Pallas kernels  51.8 us (11%)
  other arithmetic  17.2 us (4%)
  between operations  13.9 us (3%)
  local copies, waits for them, and re-layouts  10.3 us (2%)
  starting transfers between devices  9.21 us (2%)
    psum x1, waiting for transfers between devices, on_device(): lax.psum(lax.dot_general(rows, rows, (((0,), (0,)), ((), ())), preferred_...  132 us
    reduce_scatter x2, waiting for transfers between devices, summed_rows(): return lax.psum_scatter(part, 'tensor', scatter_dimension=0, tiled=True)  95.8 us
    pallas_call x1, Pallas kernels, inverse_of_lower(): pl.pallas_call(inverse_kernel, out_shape=jax.ShapeDtypeStruct((rank, rank...  51.8 us
    ppermute x1, waiting for transfers between devices, on_device(): lax.ppermute(share, 'fsdp', swap).astype(jnp.float32)  40 us
    ppermute x1, waiting for transfers between devices, on_device(): other = lax.ppermute(lowered, 'fsdp', swap)  20.4 us
    dot_general x2, matrix products, summed_rows(): jnp.dot(blended, columns, preferred_element_type=jnp.float32)  15.8 us
    dot_general x1, matrix products, on_device(): jnp.dot(orthonormal, right.astype(jnp.bfloat16), preferred_element_type=j...  15.7 us
    dot_general x1, matrix products, on_device(): lax.dot_general(orthonormal, blended, (((0,), (0,)), ((), ())), preferred...  13.8 us
  transfers between devices with their start and end apart: 10, of which 8 were waited for; matrix products, arithmetic and copies ran while one was open for 6% of the time, Pallas kernels for 11%

commit v1 on v0

v1 whole, which is shorter than its diff:
```python
import functools

import jax
import jax.numpy as jnp
from jax import lax
from jax.experimental import pallas as pl
from jax.experimental.pallas import tpu as pltpu
from jax.sharding import PartitionSpec as P

decay_rate = 0.95
epsilon = 1e-06
BLOCK = 128
HALF = 64
MESH = pl.DeviceIdType.MESH
F32 = jnp.float32
BF16 = jnp.bfloat16


def inverse_kernel(gram_ref, high_ref, low_ref, state):
    rank = gram_ref.shape[0]
    iota = functools.partial(lax.broadcasted_iota, jnp.int32)
    same = iota((rank, rank), 0) == iota((rank, rank), 1)
    diagonal = jnp.where(same, gram_ref[...], 0.0)
    scale_row = 1.0 / jnp.sqrt(jnp.sum(diagonal, axis=0, keepdims=True))
    scale_column = 1.0 / jnp.sqrt(jnp.sum(diagonal, axis=1, keepdims=True))
    state[...] = gram_ref[...] * scale_row * scale_column
    row = iota((HALF, BLOCK), 0)
    lane = iota((HALF, BLOCK), 1)
    wide_row = iota((HALF, rank), 0)
    wide = iota((HALF, rank), 1)
    exact = dict(precision=lax.Precision.HIGHEST, preferred_element_type=F32)
    over = (((0,), (0,)), ((), ()))

    @pl.loop(0, rank // HALF)
    def _(b):
        at = pl.multiple_of(b * HALF, HALF)
        tile = pl.multiple_of(b // 2 * BLOCK, BLOCK)
        odd = lax.rem(b, 2) == 1
        square = state[pl.ds(at, HALF), pl.ds(tile, BLOCK)]
        square = jnp.where(odd, pltpu.roll(square, HALF, 1), square)
        a = jnp.where(lane < HALF, square, (lane - HALF == row).astype(F32))
        for base in range(0, HALF, 8):
            now = a[base:]
            spread = [
                jnp.broadcast_to(now[:, base + k : base + k + 1], now.shape) for k in range(8)
            ]
            for k in range(0, 8 if base + 8 < HALF else 6, 2):
                first, second = spread[k], spread[k + 1]
                p = first[k : k + 1]
                q = second[k : k + 1]
                r = second[k + 1 : k + 2]
                inverse = 1.0 / (p * r - q * q)
                below = row[: HALF - base] > k + 1
                one = jnp.where(below, (first * r - second * q) * inverse, 0.0)
                two = jnp.where(below, (second * p - first * q) * inverse, 0.0)
                for n in range(k + 2, 8):
                    old = spread[n]
                    spread[n] = old - one * old[k : k + 1] - two * old[k + 1 : k + 2]
                now = now - one * now[k : k + 1] - two * now[k + 1 : k + 2]
            a = now if base == 0 else jnp.concatenate([a[:base], now], axis=0)
        above = pltpu.roll(a, 1, 0)
        left_of = lane == row - 1
        edge = jnp.sum(jnp.where(left_of, a, 0.0), axis=1, keepdims=True)
        corner = jnp.sum(jnp.where(left_of, above, 0.0), axis=1, keepdims=True)
        odd_row = lax.rem(row, 2) == 1
        a = a - jnp.where(odd_row, edge / jnp.where(odd_row, corner, 1.0), 0.0) * above
        pivots = jnp.sum(jnp.where(lane == row, a, 0.0), axis=1, keepdims=True)
        block_inverse = pltpu.roll(a * (1.0 / jnp.sqrt(pivots)), HALF, 1)[:, :HALF]
        inside = (wide >= at) & (wide < at + HALF)
        rows = jnp.where(inside, (wide - at == wide_row).astype(F32), state[pl.ds(at, HALF), :])
        solved = jnp.dot(block_inverse, rows, **exact)
        state[pl.ds(at, HALF), :] = solved
        result = jnp.where(wide < at + HALF, solved, 0.0) * scale_row
        high = result.astype(BF16)
        high_ref[pl.ds(at, HALF), :] = high
        low_ref[pl.ds(at, HALF), :] = (result - high.astype(F32)).astype(BF16)

        @pl.when(jnp.logical_not(odd))
        def _():
            later = pl.ds(pl.multiple_of(at + HALF, HALF), HALF)
            upper = pltpu.roll(state[pl.ds(at, HALF), pl.ds(tile, BLOCK)], HALF, 1)[:, :HALF]
            old = jnp.where(inside, 0.0, state[later, :])
            state[later, :] = old - lax.dot_general(upper, solved, over, **exact)

        for bb in range(rank // BLOCK - 1):

            @pl.when(b == 2 * bb + 1)
            def _():
                start, rest = bb * BLOCK, (bb + 1) * BLOCK
                pair = state[start:rest, :]
                r2 = iota(pair.shape, 0)
                c2 = iota(pair.shape, 1) - start
                dead = (r2 < HALF) & (c2 >= HALF) & (c2 < BLOCK)
                c3 = iota((rank - rest, rank), 1) - start
                old = jnp.where((c3 >= 0) & (c3 < BLOCK), 0.0, state[rest:, :])
                state[rest:, :] = old - lax.dot_general(
                    pair[:, rest:], jnp.where(dead, 0.0, pair), over, **exact
                )


def inverse_of_lower(gram):
    rank = gram.shape[0]
    vmem = pl.BlockSpec(memory_space=pltpu.VMEM)
    return pl.pallas_call(
        inverse_kernel,
        out_shape=(jax.ShapeDtypeStruct((rank, rank), BF16),) * 2,
        in_specs=[vmem],
        out_specs=(vmem, vmem),
        scratch_shapes=[pltpu.VMEM((rank, rank), F32)],
        compiler_params=pltpu.CompilerParams(vmem_limit_bytes=32 << 20),
        cost_estimate=pl.CostEstimate(flops=40_000_000_000, bytes_accessed=2 << 20, transcendentals=0),
        name="inverse",
    )(gram)


def butterfly(value, axis, size):
    if size & (size - 1):
        return lax.psum(value, axis)
    step = 1
    while step < size:
        value = value + lax.ppermute(value, axis, [(i, i ^ step) for i in range(size)])
        step *= 2
    return value


def left_kernel(
    nz,
    momentum,
    gradient,
    factor,
    blended_out,
    left_out,
    gram_out,
    w_out,
    lows,
    blended,
    stream_m,
    stream_g,
    part,
    got_a,
    sent_b,
    kept,
    got_b,
    sent_c,
    got_c,
    own,
    partial,
    left,
    w,
    gram,
    got_gram,
    in_sem,
    out_sem,
    l_sem,
    a_sem,
    b_sem,
    c_sem,
    d_sem,
    e_sem,
    f_sem,
    g_sem,
    k_sem,
):
    place = lax.axis_index("fsdp")
    t = lax.axis_index("tensor")
    c = lax.rem(t, 2)
    x = lax.rem(t // 2, 2)
    z = t // 4
    size = blended.shape[0] // (4 * nz)
    columns = w.shape[1]
    slots = stream_m.shape[0]
    per_half = columns // BLOCK
    groups = 2 * per_half
    near = range(per_half)
    far = range(per_half, groups)

    def at(zz, xx, cc):
        return place, (zz * 2 + xx) * 2 + cc

    def turned(d):
        return lax.rem(z + d, nz)

    def rows_of(cc, xx, zz):
        return pl.ds(pl.multiple_of(((cc * 2 + xx) * nz + zz) * size, size), size)

    y_peer = (1 - place, t)
    c_peer = at(z, x, 1 - c)
    x_peer = at(z, 1 - x, c)
    peers = [y_peer, c_peer, x_peer] + [at(turned(d), x, c) for d in range(1, nz)]

    def send(src, dst, sems, index, peer):
        return pltpu.make_async_remote_copy(
            src_ref=src,
            dst_ref=dst,
            send_sem=sems.at[(0,) + index],
            recv_sem=sems.at[(1,) + index],
            device_id=peer,
            device_id_type=MESH,
        )

    def position(i):
        quarter, j = i // nz, lax.rem(i, nz)
        cc = jnp.where(quarter < 2, 1 - c, c)
        xx = jnp.where(lax.rem(quarter, 2) == 0, 1 - x, x)
        return rows_of(cc, xx, lax.rem(z + 1 + j, nz))

    def fetch(i, slot):
        here = position(i)
        return (
            pltpu.make_async_copy(momentum.at[here], stream_m.at[slot], in_sem.at[0, slot]),
            pltpu.make_async_copy(gradient.at[here], stream_g.at[slot], in_sem.at[1, slot]),
        )

    chunks = 4 * nz
    for i in range(slots):
        for copy in fetch(i, i):
            copy.start()

    barrier = pltpu.get_barrier_semaphore()
    for peer in peers:
        pl.semaphore_signal(barrier, inc=1, device_id=peer, device_id_type=MESH)
    lows[0] = factor[...].astype(BF16)
    pl.semaphore_wait(barrier, len(peers))

    width = blended.shape[1]
    cut = width // 256 * 5 // 7 * 256
    pieces = (pl.ds(0, cut), pl.ds(cut, width - cut))

    def copy_l(k):
        return send(lows.at[0, pieces[k]], lows.at[1, pieces[k]], l_sem, (k,), y_peer)

    for k in range(2):
        copy_l(k).start()

    def copy_a(q, i):
        return send(part.at[q, i], got_a.at[q, i], a_sem, (q, i), c_peer)

    def copy_b(q, j):
        return send(sent_b.at[q, j], got_b.at[q, j], b_sem, (q, j), x_peer)

    def copy_c(q, d):
        return send(sent_c.at[q, d - 1], got_c.at[q, d - 1], c_sem, (q, d - 1), at(turned(d), x, c))

    def half(q):
        return place if q < per_half else 1 - place

    def spot(q):
        return half(q) * per_half + q % per_half

    def block(q, cc, xx, zz):
        return left.at[spot(q), rows_of(cc, xx, zz)]

    def copy_d(q, way, k):
        zz, to = (z - k, z + 1) if way == 0 else (z + k, z - 1)
        here = block(q, c, x, zz)
        return send(here, here, d_sem, (q, way, k), at(to, x, c))

    def can_send(way, k):
        return (z >= k) & (z < nz - 1) if way == 0 else (z + k < nz) & (z > 0)

    def copy_e(q, zz):
        here = block(q, c, x, zz)
        return send(here, here, e_sem, (q, zz), x_peer)

    def copy_f(q, side, zz):
        here = block(q, c, x if side == 0 else 1 - x, zz)
        return send(here, here, f_sem, (q, side, zz), c_peer)

    def spread(qs, i, product):
        @pl.when(i < 2 * nz)
        def _():
            for n, q in enumerate(qs):
                part[q, i] = product[:, n * BLOCK : (n + 1) * BLOCK].astype(BF16)
                copy_a(q, i).start()

        @pl.when(i >= 2 * nz)
        def _():
            j = lax.rem(i, nz)
            for n, q in enumerate(qs):
                copy_a(q, i - 2 * nz).wait_recv()
                total = product[:, n * BLOCK : (n + 1) * BLOCK] + got_a[q, i - 2 * nz].astype(F32)

                @pl.when(i < 3 * nz)
                def _():
                    sent_b[q, j] = total.astype(BF16)
                    if n == 0:
                        copy_b(q, j).start()

                @pl.when(i >= 3 * nz)
                def _():
                    kept[q, j] = total

        @pl.when(i == 3 * nz - 1)
        def _():
            for q in qs[1:]:
                for j in range(nz):
                    copy_b(q, j).start()

    def write_out(i):
        here = position(i)
        return pltpu.make_async_copy(blended.at[here], blended_out.at[here], out_sem.at[i])

    dot = functools.partial(jnp.dot, preferred_element_type=F32)

    @pl.loop(0, chunks)
    def _(i):
        slot = lax.rem(i, slots)
        for copy in fetch(i, slot):
            copy.wait()
        value = (stream_m[slot].astype(F32) + stream_g[slot].astype(F32)).astype(BF16)
        blended[position(i)] = value
        spread(near, i, dot(value, lows[0]))

        @pl.when(i + slots < chunks)
        def _():
            for copy in fetch(i + slots, slot):
                copy.start()

    @pl.loop(0, chunks)
    def _(i):
        write_out(i).start()

    def multiply_far(k, start, stop):
        @pl.loop(start // 2, stop // 2)
        def _(pair):
            both = [2 * pair, 2 * pair + 1]
            products = [dot(blended[position(i), pieces[k]], lows[1, pieces[k]]) for i in both]
            for i, product in zip(both, products):
                if k == 0:
                    partial[i] = product
                else:
                    spread(far, i, partial[i] + product)

    def take_b(q, j):
        copy_b(q, j).wait_recv()
        total = kept[q, j] + got_b[q, j].astype(F32)
        if j < nz - 1:
            sent_c[q, j] = total.astype(BF16)
            copy_c(q, j + 1).start()
        else:
            own[q] = total

    def take_c(q):
        total = own[q]
        for d in range(1, nz):
            copy_c(q, d).wait_recv()
            total = total + got_c[q, d - 1].astype(F32)
        left[spot(q), rows_of(c, x, z)] = total.astype(BF16)
        for way in range(2):

            @pl.when(can_send(way, 0))
            def _():
                copy_d(q, way, 0).start()

        copy_e(q, z).start()
        copy_f(q, 0, z).start()

    def landing(q, cc, xx, zz, sems, index):
        here = block(q, cc, xx, zz)
        return send(here, here, sems, index, c_peer)

    def at_distance(k, action):
        @pl.when(z >= k)
        def _():
            action(0, z - k)

        if k > 0:

            @pl.when(z + k < nz)
            def _():
                action(1, z + k)

    def take_d(q, k):
        def arrived(way, zz):
            landing(q, c, x, zz, d_sem, (q, way, k - 1)).wait_recv()
            if k < nz - 1:

                @pl.when(can_send(way, k))
                def _():
                    copy_d(q, way, k).start()

            copy_e(q, zz).start()
            copy_f(q, 0, zz).start()

        at_distance(k, arrived)

    def take_e(q, k):
        def arrived(way, zz):
            landing(q, c, 1 - x, zz, e_sem, (q, zz)).wait_recv()
            copy_f(q, 1, zz).start()

        at_distance(k, arrived)

    def take_f(q):
        for side in range(2):
            for zz in range(nz):
                landing(q, 1 - c, x if side == 0 else 1 - x, zz, f_sem, (q, side, zz)).wait_recv()

    over = (((0,), (0,)), ((), ()))
    step = 2 * size

    def left_rows(g, here):
        return jnp.concatenate([left[g * per_half + n, here] for n in range(per_half)], axis=1)

    steps = blended.shape[0] // step

    def right_part(h, begin, end):
        g = half(h * per_half)
        if begin == 0:
            w[g] = jnp.zeros(w.shape[1:], F32)

        @pl.loop(begin, end)
        def _(k):
            here = pl.ds(pl.multiple_of(k * step, step), step)
            w[g] += lax.dot_general(
                left_rows(g, here), blended[here], over, preferred_element_type=F32
            )

        if end == steps:
            w_out[g] = w[g].astype(BF16)

    def gram_part(index, one, two, cc):
        rows = blended.shape[0] // 2
        here = pl.ds(pl.multiple_of(cc * rows, rows), rows)
        gram[index] += lax.dot_general(
            left_rows(one, here), left_rows(two, here), over, preferred_element_type=F32
        )

    half_columns = columns // 2
    mine = pl.ds(pl.multiple_of(c * half_columns, half_columns), half_columns)
    theirs = pl.ds(pl.multiple_of((1 - c) * half_columns, half_columns), half_columns)

    def copy_g(block_index, index, got_index):
        return send(
            gram.at[block_index, mine], got_gram.at[got_index, mine], g_sem, (index,), y_peer
        )

    gram[...] = jnp.zeros(gram.shape, F32)
    q0, q1, q2, q3 = range(groups)

    def take_all_b(q):
        for j in range(nz):
            take_b(q, j)

    take_all_b(q0)
    take_c(q0)
    copy_l(0).wait_recv()
    multiply_far(0, 0, 2 * nz)
    take_all_b(q1)
    multiply_far(0, 2 * nz, chunks)
    copy_l(1).wait_recv()
    multiply_far(1, 0, 2 * nz)
    take_c(q1)
    multiply_far(1, 2 * nz, chunks)
    take_d(q0, 1)
    take_d(q0, 2)
    take_d(q1, 1)
    take_d(q0, 3)
    for j in range(nz):
        take_b(q2, j)
    take_d(q1, 2)
    take_b(q3, 0)
    take_b(q3, 1)
    take_d(q1, 3)
    take_c(q2)
    take_b(q3, 2)
    take_b(q3, 3)
    take_d(q2, 1)
    take_c(q3)
    for q in near:
        for k in range(nz):
            take_e(q, k)
    take_d(q2, 2)
    for q in near:
        take_f(q)
    right_part(0, 0, 2)
    take_d(q3, 1)
    take_d(q2, 3)
    right_part(0, 2, 4)
    gram_part(place, place, place, 0)
    take_d(q3, 2)
    gram_part(place, place, place, 1)
    copy_g(place, 0, place).start()
    right_part(0, 4, 6)
    take_d(q3, 3)
    right_part(0, 6, steps)
    for q in far:
        for k in range(nz):
            take_e(q, k)
    gram_part(1 - place, 1 - place, 1 - place, c)
    gram_part(2, 0, 1, c)
    for q in far:
        take_f(q)
    gram_part(1 - place, 1 - place, 1 - place, 1 - c)
    gram_part(2, 0, 1, 1 - c)
    copy_g(1 - place, 1, 1 - place).start()
    copy_g(2, 2, 2).start()

    def save_left(g):
        return pltpu.make_async_copy(left.at[g], left_out.at[g], k_sem.at[g])

    for g in range(groups):
        save_left(g).start()
    right_part(1, 0, steps)
    copy_g(place, 0, 1 - place).wait()
    copy_g(1 - place, 1, place).wait()
    copy_g(2, 2, 2).wait()
    gram_out[0, mine, :columns] = gram[0, mine] + got_gram[0, mine]
    gram_out[0, mine, columns:] = gram[2, mine] + got_gram[2, mine]
    gram_out[1, mine, columns:] = gram[1, mine] + got_gram[1, mine]
    gram_out[1, :, :columns] = jnp.zeros((columns, columns), F32)

    def copy_k(here, index):
        return send(gram_out.at[here], gram_out.at[here], g_sem, (index,), c_peer)

    out_k = [copy_k((0, mine), 3), copy_k((1, mine, pl.ds(columns, columns)), 4)]
    for copy in out_k:
        copy.start()

    for g in range(groups):
        save_left(g).wait()

    @pl.loop(0, chunks)
    def _(i):
        write_out(i).wait()

    for k in range(2):
        copy_l(k).wait_send()
    for q in range(groups):

        @pl.loop(0, 2 * nz)
        def _(i):
            copy_a(q, i).wait_send()

        for j in range(nz):
            copy_b(q, j).wait_send()
            copy_e(q, j).wait_send()
            copy_f(q, 0, j).wait_send()
            copy_f(q, 1, j).wait_send()
            if j > 0:
                copy_c(q, j).wait_send()
            if j < nz - 1:
                for way in range(2):

                    @pl.when(can_send(way, j))
                    def _():
                        copy_d(q, way, j).wait_send()

    copy_k((0, theirs), 3).wait_recv()
    copy_k((1, theirs, pl.ds(columns, columns)), 4).wait_recv()
    for copy in out_k:
        copy.wait_send()


def left_stage(nz, momentum, gradient, factor):
    rows, width = momentum.shape
    columns = factor.shape[1]
    size = rows // (4 * nz)
    groups = 2 * columns // BLOCK
    slots = 4
    dma = pltpu.SemaphoreType.DMA
    vmem = pl.BlockSpec(memory_space=pltpu.VMEM)
    anywhere = pl.BlockSpec(memory_space=pl.ANY)
    return pl.pallas_call(
        functools.partial(left_kernel, nz),
        out_shape=(
            jax.ShapeDtypeStruct((rows, width), BF16),
            jax.ShapeDtypeStruct((groups, rows, BLOCK), BF16),
            jax.ShapeDtypeStruct((2, columns, 2 * columns), F32),
            jax.ShapeDtypeStruct((2, columns, width), BF16),
        ),
        in_specs=[anywhere, anywhere, vmem],
        out_specs=(anywhere, anywhere, vmem, vmem),
        scratch_shapes=[
            pltpu.VMEM((2, width, columns), BF16),
            pltpu.VMEM((rows, width), BF16),
            pltpu.VMEM((slots, size, width), BF16),
            pltpu.VMEM((slots, size, width), BF16),
            pltpu.VMEM((groups, 2 * nz, size, BLOCK), BF16),
            pltpu.VMEM((groups, 2 * nz, size, BLOCK), BF16),
            pltpu.VMEM((groups, nz, size, BLOCK), BF16),
            pltpu.VMEM((groups, nz, size, BLOCK), F32),
            pltpu.VMEM((groups, nz, size, BLOCK), BF16),
            pltpu.VMEM((groups, nz - 1, size, BLOCK), BF16),
            pltpu.VMEM((groups, nz - 1, size, BLOCK), BF16),
            pltpu.VMEM((groups, size, BLOCK), F32),
            pltpu.VMEM((4 * nz, size, columns), F32),
            pltpu.VMEM((groups, rows, BLOCK), BF16),
            pltpu.VMEM((2, columns, width), F32),
            pltpu.VMEM((3, columns, columns), F32),
            pltpu.VMEM((3, columns, columns), F32),
            dma((2, slots)),
            dma((4 * nz,)),
            dma((2, 2)),
            dma((2, groups, 2 * nz)),
            dma((2, groups, nz)),
            dma((2, groups, nz - 1)),
            dma((2, groups, 2, nz - 1)),
            dma((2, groups, nz)),
            dma((2, groups, 2, nz)),
            dma((2, 5)),
            dma((groups,)),
        ],
        compiler_params=pltpu.CompilerParams(
            collective_id=0, has_side_effects=True, vmem_limit_bytes=56 << 20
        ),
        name="left",
    )(momentum, gradient, factor)


def right_kernel(
    n, high, low, w, other, left, orthonormal, right_out, normal_out, own_out, right, sums, s_sem
):
    place = lax.axis_index("fsdp")
    t = lax.axis_index("tensor")
    rank, width = right.shape
    columns = own_out.shape[0]
    per_half = columns // BLOCK

    def peer(d):
        return place, lax.rem(t + d, n)

    def copy(d):
        return pltpu.make_async_remote_copy(
            src_ref=sums.at[0],
            dst_ref=sums.at[d],
            send_sem=s_sem.at[0, d],
            recv_sem=s_sem.at[1, d],
            device_id=peer(d),
            device_id_type=MESH,
        )

    barrier = pltpu.get_barrier_semaphore()

    @pl.loop(1, n)
    def _(d):
        pl.semaphore_signal(barrier, inc=1, device_id=peer(d), device_id_type=MESH)

    dot = functools.partial(jnp.dot, preferred_element_type=F32)
    squares = jnp.zeros((rank, BLOCK), F32)
    for start in range(0, width, 2 * BLOCK):
        here = slice(start, start + 2 * BLOCK)
        total = w[:, here].astype(F32) + other[:, here].astype(F32)
        w_high = total.astype(BF16)
        w_low = (total - w_high.astype(F32)).astype(BF16)
        value = dot(high[...], w_high) + dot(high[...], w_low) + dot(low[...], w_high)
        right[:, here] = value
        value = value * value
        squares = squares + value[:, :BLOCK] + value[:, BLOCK:]
    sums[0] = jnp.sum(squares.T, axis=0, keepdims=True)
    pl.semaphore_wait(barrier, n - 1)

    @pl.loop(1, n)
    def _(d):
        copy(d).start()

    right_out[...] = right[...].astype(BF16)
    size = 256
    across = (((1,), (1,)), ((), ()))

    @pl.loop(0, left.shape[1] // size)
    def _(i):
        here = pl.ds(pl.multiple_of(i * size, size), size)
        total = None
        for g in range(2):
            rows = jnp.concatenate([left[g * per_half + n, here] for n in range(per_half)], axis=1)
            for piece in (high, low):
                term = lax.dot_general(
                    rows,
                    piece[:, g * columns : (g + 1) * columns],
                    across,
                    preferred_element_type=F32,
                )
                total = term if total is None else total + term
        orthonormal[here] = total.astype(BF16)

    @pl.loop(1, n)
    def _(d):
        copy(d).wait()

    square_sums = sums[0]
    for d in range(1, n):
        square_sums = square_sums + sums[d]
    inverse = jnp.broadcast_to(lax.rsqrt(square_sums + epsilon), (BLOCK, rank)).T
    for start in range(0, width, BLOCK):
        here = slice(start, start + BLOCK)
        right[:, here] = right[:, here] * inverse
    normal_out[...] = right[...].astype(BF16)
    own_out[...] = right[pl.ds(pl.multiple_of(place * columns, columns), columns)]


def right_stage(n, high, low, w, other, left):
    rank, width = w.shape
    rows = left.shape[1]
    columns = rank // 2
    vmem = pl.BlockSpec(memory_space=pltpu.VMEM)
    return pl.pallas_call(
        functools.partial(right_kernel, n),
        out_shape=(
            jax.ShapeDtypeStruct((rows, rank), BF16),
            jax.ShapeDtypeStruct((rank, width), BF16),
            jax.ShapeDtypeStruct((rank, width), BF16),
            jax.ShapeDtypeStruct((columns, width), F32),
        ),
        in_specs=[vmem] * 5,
        out_specs=(vmem,) * 4,
        scratch_shapes=[
            pltpu.VMEM((rank, width), F32),
            pltpu.VMEM((n, 1, rank), F32),
            pltpu.SemaphoreType.DMA((2, n)),
        ],
        compiler_params=pltpu.CompilerParams(
            collective_id=1, has_side_effects=True, vmem_limit_bytes=32 << 20
        ),
        cost_estimate=pl.CostEstimate(flops=8_000_000_000, bytes_accessed=16 << 20, transcendentals=0),
        name="right",
    )(high, low, w, other, left)


def output_kernel(scale, orthonormal, blended, right, normal, own, momentum_out, update_out, factor_out):
    product = jnp.dot(orthonormal[...], right[...], preferred_element_type=F32)
    momentum_out[...] = (blended[...].astype(F32) - (1.0 - decay_rate) * product).astype(BF16)
    stepped = jnp.dot(orthonormal[...], normal[...], preferred_element_type=F32)
    update_out[...] = (stepped * scale).astype(BF16)
    factor_out[...] = own[...].T


def output_stage(scale, orthonormal, blended, right, normal, own):
    rows, width = blended.shape
    rank = orthonormal.shape[1]
    columns = own.shape[0]
    size = 256
    last = width // BLOCK - 1
    whole = pl.BlockSpec((rank, width), lambda i: (0, 0), pipeline_mode=pl.Buffered(1))
    chunk = pl.BlockSpec((size, width), lambda i: (i, 0))
    return pl.pallas_call(
        functools.partial(output_kernel, scale),
        grid=(rows // size,),
        out_shape=(jax.ShapeDtypeStruct((rows, width), BF16),) * 2
        + (jax.ShapeDtypeStruct((width, columns), F32),),
        in_specs=[
            pl.BlockSpec((size, rank), lambda i: (i, 0)),
            chunk,
            whole,
            whole,
            pl.BlockSpec((columns, BLOCK), lambda i: (0, jnp.minimum(i, last))),
        ],
        out_specs=(chunk, chunk, pl.BlockSpec((BLOCK, columns), lambda i: (jnp.minimum(i, last), 0))),
        compiler_params=pltpu.CompilerParams(
            dimension_semantics=("arbitrary",), vmem_limit_bytes=40 << 20
        ),
        name="outputs",
    )(orthonormal, blended, right, normal, own)


def paired(halves, spread, momentum, gradient, factor):
    whole_rows = momentum.shape[0] * halves
    whole_columns = momentum.shape[1] * spread
    rank = factor.shape[1] * halves

    blended, left, gram, w = left_stage(spread // 4, momentum, gradient, factor)
    w = w.reshape(rank, w.shape[2])
    other = lax.ppermute(w, "fsdp", [(0, 1), (1, 0)])
    high, low = inverse_of_lower(gram.reshape(rank, rank))
    orthonormal, right, normal, own = right_stage(spread, high, low, w, other, left)
    scale = (whole_rows * whole_columns / rank) ** 0.5
    new_momentum, update, new_factor = output_stage(scale, orthonormal, blended, right, normal, own)
    return (new_momentum, new_factor, update)


def general(halves, spread, momentum, gradient, factor):
    whole_rows = momentum.shape[0] * halves
    whole_columns = momentum.shape[1] * spread
    own_rank = factor.shape[1]
    rank = own_rank * halves
    place = lax.axis_index("fsdp")

    blended = (momentum.astype(jnp.float32) + gradient.astype(jnp.float32)).astype(jnp.bfloat16)
    lowered = lax.all_gather(factor.astype(jnp.bfloat16), "fsdp", axis=1, tiled=True)
    part = jnp.dot(blended, lowered, preferred_element_type=jnp.float32).astype(jnp.bfloat16)
    rows = lax.psum_scatter(part, "tensor", scatter_dimension=0, tiled=True)

    gram = lax.psum(
        lax.dot_general(rows, rows, (((0,), (0,)), ((), ())), preferred_element_type=jnp.float32),
        ("fsdp", "tensor"),
    )
    left = lax.all_gather(rows, "tensor", axis=0, tiled=True)
    high, low = inverse_of_lower(gram)
    across = (((1,), (1,)), ((), ()))
    orthonormal = (
        lax.dot_general(left, high, across, preferred_element_type=jnp.float32)
        + lax.dot_general(left, low, across, preferred_element_type=jnp.float32)
    ).astype(jnp.bfloat16)

    share = lax.dot_general(
        orthonormal, blended, (((0,), (0,)), ((), ())), preferred_element_type=jnp.float32
    ).astype(jnp.bfloat16)
    right = lax.psum(share, "fsdp").astype(jnp.float32)
    square_sums = butterfly(jnp.sum(right * right, axis=1), "tensor", spread)
    inverse = lax.rsqrt(square_sums + epsilon)
    normal = right * inverse[:, None]
    own_factor = lax.dynamic_slice_in_dim(normal, place * own_rank, own_rank, axis=0).T
    product = jnp.dot(orthonormal, right.astype(jnp.bfloat16), preferred_element_type=jnp.float32)
    new_momentum = (blended.astype(jnp.float32) - (1.0 - decay_rate) * product).astype(jnp.bfloat16)
    stepped = jnp.dot(orthonormal, normal.astype(jnp.bfloat16), preferred_element_type=jnp.float32)
    scale = jnp.sqrt(jnp.float32(whole_rows * whole_columns / rank))
    update = (stepped * scale).astype(jnp.bfloat16)
    return (new_momentum, own_factor, update)


def solution(mesh):
    halves, spread = mesh.shape["fsdp"], mesh.shape["tensor"]

    def body(momentum, gradient, factor):
        rows, width = momentum.shape
        fits = rows % (2 * spread * BLOCK) == 0 and width % (2 * BLOCK) == 0
        fits = fits and factor.shape[1] == 2 * BLOCK and width // BLOCK <= rows // (2 * BLOCK)
        paired_mesh = halves == 2 and spread == 16
        on_device = paired if paired_mesh and fits else general
        return on_device(halves, spread, momentum, gradient, factor)

    return jax.shard_map(
        body,
        mesh=mesh,
        in_specs=(P("fsdp", "tensor"), P("fsdp", "tensor"), P("tensor", "fsdp")),
        out_specs=(P("fsdp", "tensor"), P("tensor", "fsdp"), P("fsdp", "tensor")),
        check_vma=False,
    )
```

time: 462 us -> 164 us (0.35)
  waiting for transfers between devices: 295 us -> 19.5 us
  Pallas kernels: 51.8 us -> 141 us
  matrix products: 64.4 us -> 0 us
  other arithmetic: 17.2 us -> 0 us
  between operations: 13.9 us -> 0.66 us
  local copies, waits for them, and re-layouts: 10.3 us -> 1.23 us
  starting transfers between devices: 9.21 us -> 0.42 us
    psum x1 -> x0, waiting for transfers between devices: 132 us -> none  [on_device(): lax.psum(lax.dot_general(rows, rows, (((0,), (0,)), ((), ())), preferred_...]
    reduce_scatter x2 -> x0, waiting for transfers between devices: 95.8 us -> none  [summed_rows(): return lax.psum_scatter(part, 'tensor', scatter_dimension=0, tiled=True)]
    pallas_call x1 -> x4, Pallas kernels: 51.8 us -> 141 us  [the longest x1 82.3 us: left_stage(): pl.pallas_call(functools.partial(left_kernel, nz), out_shape=(jax.ShapeDt...]
    dot_general x8 -> x0, matrix products: 64.4 us -> none  [the longest x2 15.8 us: summed_rows(): jnp.dot(blended, columns, preferred_element_type=jnp.float32)]
    ppermute x6 -> x1, waiting for transfers between devices: 66.2 us -> 19.5 us  [paired(): other = lax.ppermute(w, 'fsdp', [(0, 1), (1, 0)])]
    convert_element_type x2 -> x0, other arithmetic: 13.2 us -> none  [the longest x1 11.6 us: on_device(): (momentum.astype(jnp.float32) + gradient.astype(jnp.float32)).astype(jnp....]
    unnamed x15 -> x6, local copies, waits for them, and re-layouts: 10.2 us -> 1.23 us
    ppermute x6 -> x1, starting transfers between devices: 8.87 us -> 0.42 us  [paired(): other = lax.ppermute(w, 'fsdp', [(0, 1), (1, 0)])]
  transfers between devices with their start and end apart: 10 -> 1, of which waited for: 8 -> 1; matrix products, arithmetic and copies ran while one was open for 6% -> 0% of each run, Pallas kernels for 11% -> 13%
where the time goes in v1:
time: 164 us; the launch traced here: 163 us
  Pallas kernels  141 us (86%)
  waiting for transfers between devices  19.5 us (12%)
    pallas_call x1, Pallas kernels, left_stage(): pl.pallas_call(functools.partial(left_kernel, nz), out_shape=(jax.ShapeDt...  82.3 us
    pallas_call x1, Pallas kernels, output_stage(): pl.pallas_call(functools.partial(output_kernel, scale), grid=(rows // siz...  25.2 us
    pallas_call x1, Pallas kernels, inverse_of_lower(): pl.pallas_call(inverse_kernel, out_shape=(jax.ShapeDtypeStruct((rank, ran...  21.4 us
    ppermute x1, waiting for transfers between devices, paired(): other = lax.ppermute(w, 'fsdp', [(0, 1), (1, 0)])  19.5 us
    pallas_call x1, Pallas kernels, right_stage(): pl.pallas_call(functools.partial(right_kernel, n), out_shape=(jax.ShapeDt...  12.4 us
  transfers between devices with their start and end apart: 1, of which 1 were waited for; matrix products, arithmetic and copies ran while one was open for 0% of the time, Pallas kernels for 13%

profile of v1, /device:TPU:0, one launch (start us, length us, event | category | flops | bytes accessed | tf_op | source)
XLA Modules:
  0.0 163.1 jit_solution(9248457501570293896)
XLA Ops:
  0.6 82.3 %left.1 = (bf16[4096,1792]{1,0:T(8,128)(2,1)}, bf16[4,4096,128]{2,1,0:T(8,128)(2,1)}, f32[2,256,512]{2,1,0:T(8,128)}, bf16[2,256,1792]{2,1,0:T(8,128)(2,1)}) custom-call(bf16[4096,1792]{1,0:T(8,128)(2,1)} %momentum.1, bf16[4096,1792]{1,0:T(8,128)(2,1)} %gradient.1, f32[1792,256]{1,0:T(8,128)} %factor.1), custom_call_target="tpu_custom_call" | custom-call | tf_op jit(solution)/shard_map/left/pallas_call | solution.py:564
  82.9 0.4 collective-permute-start
  83.4 0.0 copy-start.2
  83.4 1.2 copy-done.2
  84.6 0.0 copy-start
  84.6 0.0 copy-start.1
  84.6 21.4 %inverse.1 = (bf16[512,512]{1,0:T(8,128)(2,1)S(1)}, bf16[512,512]{1,0:T(8,128)(2,1)S(1)}) custom-call(f32[512,512]{1,0:T(8,128)S(1)} %bitcast.4), custom_call_target="tpu_custom_call" | custom-call | flops 40000000000 | bytes 2097152 | tf_op jit(solution)/shard_map/inverse/pallas_call | solution.py:104
  106.0 19.5 %collective-permute-done.other = bf16[512,1792]{1,0:T(8,128)(2,1)S(1)} collective-permute-done((bf16[512,1792]{1,0:T(8,128)(2,1)}, bf16[512,1792]{1,0:T(8,128)(2,1)S(1)}, u32[]{:S(2)}, u32[]{:S(2)}) %collective-permute-start) | collective-permute-done | bytes 1835040 | tf_op jit(solution)/shard_map/ppermute | solution.py:763
  125.5 0.0 copy-done
  125.5 0.0 copy-done.1
  125.5 12.4 %right.1 = (bf16[4096,512]{1,0:T(8,128)(2,1)S(1)}, bf16[512,1792]{1,0:T(8,128)(2,1)S(1)}, bf16[512,1792]{1,0:T(8,128)(2,1)S(1)}, f32[256,1792]{1,0:T(8,128)S(1)}) custom-call(bf16[512,512]{1,0:T(8,128)(2,1)S(1)} %get-tuple-element.17.high, bf16[512,512]{1,0:T(8,128)(2,1)S(1)} %get-tuple-element.18.low, bf16[512,1792]{1,0:T(8,128)(2,1)S(1)} %bitcast.3, ...), custom_call_target="tpu_custom_call" | custom-call | flops 8000000000 | bytes 16777216 | tf_op jit(solution)/shard_map/right/pallas_call | solution.py:697
  137.9 25.2 %outputs.1 = (bf16[4096,1792]{1,0:T(8,128)(2,1)}, bf16[4096,1792]{1,0:T(8,128)(2,1)}, f32[1792,256]{1,0:T(8,128)}) custom-call(bf16[4096,512]{1,0:T(8,128)(2,1)S(1)} %get-tuple-element.21.orthonormal, bf16[4096,1792]{1,0:T(8,128)(2,1)} %get-tuple-element.22.blended, bf16[512,1792]{1,0:T(8,128)(2,1)S(1)} %get-tuple-element.23.right, ...), custom_call_target="tpu_custom_call" | custom-call | tf_op jit(solution)/shard_map/outputs/pallas_call | solution.py:736
Async XLA Ops:
  82.9 42.6 %collective-permute-start = (bf16[512,1792]{1,0:T(8,128)(2,1)}, bf16[512,1792]{1,0:T(8,128)(2,1)S(1)}, u32[]{:S(2)}, u32[]{:S(2)}) collective-permute-start(bf16[512,1792]{1,0:T(8,128)(2,1)} %bitcast.2), channel_id=1, source_target_pairs={{0,16},{16,0},{1,17},{17,1},{2,18},{18,2},{3,19},{19,3},{4,20},{20... | collective-permute-start | bytes 5505032 | tf_op jit(solution)/shard_map/ppermute | solution.py:763
  83.4 1.2 copy-start.2
  84.6 40.9 %copy-start = (bf16[4,4096,128]{2,1,0:T(8,128)(2,1)S(1)}, bf16[4,4096,128]{2,1,0:T(8,128)(2,1)}, u32[]{:S(2)}) copy-start(bf16[4,4096,128]{2,1,0:T(8,128)(2,1)} %get-tuple-element.20.left) | copy-start | bytes 12582916
  84.6 40.9 %copy-start.1 = (bf16[2,256,1792]{2,1,0:T(8,128)(2,1)S(1)}, bf16[2,256,1792]{2,1,0:T(8,128)(2,1)}, u32[]{:S(2)}) copy-start(bf16[2,256,1792]{2,1,0:T(8,128)(2,1)} %get-tuple-element.19) | copy-start | bytes 5505028
